TPU v7x, 32 devices: a whole 2x2x4 slice. The times are simulated.
32 devices in a mesh: fsdp: 4 (over y, x), tp: 2 (over core), rep: 4 (over z).
Axes of the slice: x: 2, y: 2, z: 4, core: 2. Of those that a mesh axis runs over, the one named last changes fastest.
Arguments:
- tokens: bfloat16 [4096, 5120], P('fsdp', 'rep'), may hold values from -6 to 6
- ref_qkv: bfloat16 [5120, 7168], P(('rep', 'fsdp'), 'tp'), may hold values from -0.078125 to 0.078125
- ref_bias: float32 [7168], P('tp'), may hold values from -9 to 9
- segment_ids: int32 [4, 1024], P('fsdp'), may hold values from 0 to 7, never falling along the last dimension, each value on 1 to 512 neighbouring positions
- policy_key: bfloat16 [5120, 1024], P(('rep', 'fsdp'), 'tp'), may hold values from -0.078125 to 0.078125
Outputs:
- context: bfloat16 [4096, 5120], P(('fsdp', 'rep'), 'tp')
- policy_key_tp: bfloat16 [5120, 1024], P(None, 'tp')
All inputs are finite; a program needn't handle non-finite values.
Results may differ from a plain program's by a relative error of at most 0.0093.
Values may be sent and summed in bfloat16 or wider, within the bound.
A program may use at most 128 MiB of HBM per device.

v0:
```python
import jax
import jax.numpy as jnp
from jax import lax
from jax.experimental import pallas as pl
from jax.experimental.pallas import tpu as pltpu
from jax.sharding import PartitionSpec as P
import functools
import math

MESH = pl.DeviceIdType.MESH

QH = 40
KVH = 8
HD = 128


def positions_of(seg):
    count = seg.shape[0]
    index = jnp.arange(count, dtype=jnp.int32)
    starts = jnp.concatenate([jnp.ones((1,), bool), seg[1:] != seg[:-1]])
    first = lax.cummax(jnp.where(starts, index, 0), axis=0)
    return index - first


def rotary(values, pos):
    half = values.shape[-1] // 2
    freq = 1000000.0 ** (-2.0 * jnp.arange(half, dtype=jnp.float32) / values.shape[-1])
    angle = pos.astype(jnp.float32)[:, None] * freq[None, :]
    shape = (values.shape[0],) + (1,) * (values.ndim - 2) + (half,)
    cosine = jnp.cos(angle).reshape(shape)
    sine = jnp.sin(angle).reshape(shape)
    first = values[..., :half]
    second = values[..., half:]
    return jnp.concatenate(
        [first * cosine - second * sine, second * cosine + first * sine], axis=-1
    )


def per_device(tokens, ref_qkv, ref_bias, segment_ids, policy_key):
    share = QH // KVH
    rows = tokens.shape[0]
    columns = ref_qkv.shape[1]
    groups = columns // ((share + 2) * HD)
    replicas = lax.axis_size("rep")
    mine = rows // replicas
    rank = lax.axis_index("rep")
    partial_value = jnp.dot(
        tokens,
        lax.all_gather(ref_qkv, "fsdp", axis=0, tiled=True),
        preferred_element_type=jnp.float32,
    )
    partial_value = partial_value.reshape(rows, groups, share + 2, HD)
    bias = ref_bias.reshape(groups, share + 2, HD)
    seg = segment_ids[0]
    pos = positions_of(seg)
    start = rank * mine
    my_pos = lax.dynamic_slice_in_dim(pos, start, mine, 0)
    summed = lax.psum_scatter(partial_value, "rep", scatter_dimension=0, tiled=True) + bias[None]
    query = rotary(summed[:, :, :share], my_pos).astype(jnp.bfloat16)
    my_keys = rotary(summed[:, :, share], my_pos).astype(jnp.bfloat16)
    my_vals = summed[:, :, share + 1].astype(jnp.bfloat16)
    keys, vals = (
        lax.all_gather(my_keys, "rep", axis=0, tiled=True),
        lax.all_gather(my_vals, "rep", axis=0, tiled=True),
    )
    scores = jnp.einsum(
        "qhgd,khd->hgqk", query, keys, preferred_element_type=jnp.float32
    ) / jnp.sqrt(jnp.float32(HD))
    query_index = start + jnp.arange(mine, dtype=jnp.int32)
    key_index = jnp.arange(rows, dtype=jnp.int32)
    my_seg = lax.dynamic_slice_in_dim(seg, start, mine, 0)
    allowed = (my_seg[:, None] == seg[None, :]) & (key_index[None, :] <= query_index[:, None])
    scores = jnp.where(allowed[None, None], scores, -1e30)
    top = jnp.max(scores, axis=-1, keepdims=True)
    expo = jnp.exp(scores - top)
    weights = (expo / jnp.sum(expo, axis=-1, keepdims=True)).astype(jnp.bfloat16)
    context = jnp.einsum("hgqk,khd->qhgd", weights, vals, preferred_element_type=jnp.float32)
    context = context.astype(jnp.bfloat16).reshape(mine, groups * share * HD)
    inner = lax.all_gather(policy_key, "rep", axis=0, tiled=True)
    outer = lax.all_gather(inner, "fsdp", axis=0, tiled=True)
    blocks = policy_key.shape[0]
    shards = outer.shape[0] // (blocks * replicas)
    whole = (
        outer.reshape(shards, replicas, blocks, outer.shape[1])
        .transpose(1, 0, 2, 3)
        .reshape(outer.shape)
    )
    return (context, whole)


def neighbours():
    f, r, t = lax.axis_index("fsdp"), lax.axis_index("rep"), lax.axis_index("tp")
    ahead = [{"rep": lax.rem(r + k, 4)} for k in range(4)]
    fx = f - lax.rem(f, 2) + 1 - lax.rem(f, 2)
    fy = lax.rem(f + 2, 4)
    return f, r, t, ahead, fx, fy


def greet(devices):
    barrier = pltpu.get_barrier_semaphore()
    for device in devices:
        pl.semaphore_signal(barrier, inc=1, device_id=device, device_id_type=MESH)
    pl.semaphore_wait(barrier, len(devices))


class Copies:
    def __init__(self, send, recv):
        self.send, self.recv, self.made = send, recv, []

    def start(self, src, dst, device, sends=None):
        n = len(self.made)
        copy = pltpu.make_async_remote_copy(
            src_ref=src, dst_ref=dst, send_sem=self.send.at[n], recv_sem=self.recv.at[n],
            device_id=device, device_id_type=MESH,
        )
        only(sends, copy.start)
        self.made.append((copy, sends))
        return copy

    def finish(self):
        for copy, sends in self.made:
            only(sends, copy.wait_send)


def only(condition, act):
    if condition is None:
        act()
    else:
        pl.when(condition)(act)


N_COPIES = 57


def layer_kernel(
    tok, w, bias, cosine, sine, seg_col, seg_row, pol, out, pg,
    x, wg, proj, keys, vals, ctx, send, recv, local, ctx_send, ctx_recv,
):
    f, r, t, ahead, fx, fy = neighbours()
    to_x, to_y, partner = {"fsdp": fx}, {"fsdp": fy}, {"tp": 1 - t}
    greet([ahead[1], ahead[2], ahead[3], to_x, to_y, partner])
    copies = Copies(send, recv)
    rows, depth = tok.shape
    mine, half = rows // 4, rows // 2
    block, width = w.shape[0], wg.shape[2]
    hb = block // 2
    share = width // HD - 2
    pw = pol.shape[1] // 2
    lo, hi = pl.ds(0, pw), pl.ds(pw, pw)
    top, low = pl.ds(0, hb), pl.ds(hb, hb)
    source = [lax.rem(r + 4 - k, 4) for k in range(4)]

    def cols(rank):
        return pl.ds(pl.multiple_of(rank * width, 128), width)

    def held(k, owner, first, count):
        return wg.at[source[k], pl.ds(pl.multiple_of(owner * block + first, 16), count)]

    def across(src, k):
        dst = held(k, f, 0, block)
        return copies.start(src, dst, to_x), copies.start(src, dst, to_y)

    def onward(k):
        bx, by = passed[k]
        bx.wait_recv()
        a = copies.start(held(k, fx, 0, hb), held(k, fx, 0, hb), to_y)
        by.wait_recv()
        b = copies.start(held(k, fy, hb, hb), held(k, fy, hb, hb), to_x)
        return [a, b]

    def policy_z(c):
        return [copies.start(pol.at[:, c], pg.at[r, f, :, c], ahead[k]) for k in (1, 3, 2)]

    def policy_xy(c, arrived):
        for copy in arrived:
            copy.wait_recv()
        src = pg.at[:, f, :, c]
        return copies.start(src, src, to_x), copies.start(src, src, to_y)

    def policy_last(c, pair):
        a, b = pg.at[:, fx, top, c], pg.at[:, fy, low, c]
        pair[0].wait_recv()
        one = copies.start(a, a, to_y)
        pair[1].wait_recv()
        return [one, copies.start(b, b, to_x)]

    parts = [pl.ds(pl.multiple_of(c * half + t * mine, mine), mine) for c in range(2)]

    def line(k, c):
        part = parts[c]
        below, above = source[k - 1], lax.rem(r + k - 1, 4)
        up_src = tok.at[part] if k == 1 else x.at[below, part]
        down_src = tok.at[part] if k == 1 else x.at[above, part]
        up = copies.start(up_src, x.at[below, part], ahead[1], (r <= 2) & (r >= k - 1))
        down = copies.start(down_src, x.at[above, part], ahead[3], (r >= 1) & (r <= 4 - k))
        return up, down

    def landed(k, pair):
        only(r >= k, pair[0].wait_recv)
        only(r <= 3 - k, pair[1].wait_recv)

    def to_partner(k, c):
        part = parts[c]
        below, above = x.at[source[k], part], x.at[lax.rem(r + k, 4), part]
        return (
            copies.start(below, below, partner, r >= k),
            copies.start(above, above, partner, r <= 3 - k),
        )

    def add(left, plane, c):
        def tile(i, _):
            at = pl.ds(pl.multiple_of(c * half + i * mine, mine), mine)
            proj[at, :] += jnp.dot(left[at, :], wg[plane], preferred_element_type=jnp.float32)
            return 0

        lax.fori_loop(0, 2, tile, 0)

    def add_planes(k, pair, c):
        def below():
            pair[0].wait_recv()
            add(x.at[source[k]], source[k], c)

        def above():
            pair[1].wait_recv()
            add(x.at[lax.rem(r + k, 4)], lax.rem(r + k, 4), c)

        only(r >= k, below)
        only(r <= 3 - k, above)

    own_w = pltpu.make_async_copy(w.at[:, cols(r)], held(0, f, 0, block), local.at[0])
    own_p = pltpu.make_async_copy(pol, pg.at[r, f], local.at[1])
    passed = {0: across(w.at[:, cols(r)], 0)}
    spread = {
        k: copies.start(w.at[:, cols(lax.rem(r + k, 4))], wg.at[r, pl.ds(pl.multiple_of(f * block, 16), block)], ahead[k])
        for k in (1, 3, 2)
    }
    lo_z = policy_z(lo)
    hi_z = policy_z(hi)
    near = line(1, 0)
    near_late = line(1, 1)
    own_w.start()
    own_p.start()
    proj[...] = jnp.broadcast_to(bias[...], proj.shape)
    for k in (1, 3):
        spread[k].wait_recv()
        passed[k] = across(held(k, f, 0, block), k)
    weights_in = onward(0)
    spread[2].wait_recv()
    passed[2] = across(held(2, f, 0, block), 2)
    weights_in += onward(1)
    weights_in += onward(3)
    landed(1, near)
    mid = line(2, 0)
    shared_near = to_partner(1, 0)
    weights_in += onward(2)
    own_p.wait()
    lo_xy = policy_xy(lo, lo_z)
    hi_xy = policy_xy(hi, hi_z)
    own_w.wait()
    for copy in weights_in[:2]:
        copy.wait_recv()
    landed(1, near_late)
    mid_late = line(2, 1)
    shared_near_late = to_partner(1, 1)
    add(tok, r, 0)
    add(tok, r, 1)
    landed(2, mid)
    far = line(3, 0)
    shared_mid = to_partner(2, 0)
    for copy in weights_in[2:]:
        copy.wait_recv()
    add_planes(1, shared_near, 0)
    rest = policy_last(lo, lo_xy)
    add_planes(2, shared_mid, 0)
    landed(2, mid_late)
    far_late = line(3, 1)
    shared_mid_late = to_partner(2, 1)
    add_planes(1, shared_near_late, 1)
    rest += policy_last(hi, hi_xy)
    landed(3, far)
    add_planes(3, to_partner(3, 0), 0)

    def rotated(values, at):
        return values * cosine[at, :] + pltpu.roll(values, HD // 2, 1) * sine[at, :]

    def column(j):
        return pl.ds(pl.multiple_of(j * HD, HD), HD)

    scale = 1.0 / math.sqrt(HD)

    def rotate_keys(i):
        at = pl.ds(i * mine, mine)
        keys[at, :] = rotated(proj[at, column(share)], at).astype(jnp.bfloat16)
        vals[at, :] = proj[at, column(share + 1)].astype(jnp.bfloat16)

    place = pl.ds(pl.multiple_of(r * share * HD, HD), share * HD)
    own_c = pltpu.make_async_copy(ctx.at[r], out.at[:, place], local.at[2])

    def send_context(d, step):
        return pltpu.make_async_remote_copy(
            src_ref=ctx.at[d], dst_ref=out.at[:, place],
            send_sem=ctx_send.at[step], recv_sem=ctx_recv.at[step],
            device_id={"rep": d}, device_id_type=MESH,
        )

    def attend(d):
        first = max(d - 2, 0)
        q0, k0, span = d * mine, first * mine, (d + 1 - first) * mine
        at, window = pl.ds(q0, mine), pl.ds(k0, span)
        q_index = q0 + lax.broadcasted_iota(jnp.int32, (mine, span), 0)
        k_index = k0 + lax.broadcasted_iota(jnp.int32, (mine, span), 1)
        allowed = (seg_col[at, :] == seg_row[:, window]) & (k_index <= q_index)
        shut = jnp.where(allowed, 0.0, -1e30)
        kk, vv = keys[window, :], vals[window, :]

        def head(j, _):
            c = column(j)
            query = rotated(proj[at, c], at).astype(jnp.bfloat16)
            scores = lax.dot_general(
                query, kk, (((1,), (1,)), ((), ())), preferred_element_type=jnp.float32
            ) * scale + shut
            expo = jnp.exp(scores - jnp.max(scores, axis=-1, keepdims=True))
            total = jnp.sum(expo, axis=-1, keepdims=True)
            weights = (expo * (1.0 / total)).astype(jnp.bfloat16)
            ctx[d, :, c] = jnp.dot(weights, vv, preferred_element_type=jnp.float32).astype(jnp.bfloat16)
            return 0

        lax.fori_loop(0, share, head, 0)

        pl.when(r == d)(own_c.start)
        pl.when(r != d)(send_context(d, lax.rem(d + 4 - r, 4)).start)

    rotate_keys(0)
    attend(0)
    rotate_keys(1)
    attend(1)
    add_planes(2, shared_mid_late, 1)
    landed(3, far_late)
    add_planes(3, to_partner(3, 1), 1)
    rotate_keys(2)
    rotate_keys(3)
    attend(3)
    attend(2)
    for copy in rest:
        copy.wait_recv()
    own_c.wait()
    for k in (1, 2, 3):
        copy = send_context(lax.rem(r + k, 4), k)
        copy.wait_send()
        copy.wait_recv()
    copies.finish()


def whole_layer(tokens, ref_qkv, bias, cosine, sine, seg, policy_key):
    rows, depth = tokens.shape
    block, columns = ref_qkv.shape
    width = columns // 4
    mine, share = rows // 4, width // HD - 2
    any_space = pl.BlockSpec(memory_space=pl.ANY)
    out, pg = pl.pallas_call(
        layer_kernel,
        out_shape=(
            jax.ShapeDtypeStruct((mine, 4 * share * HD), jnp.bfloat16),
            jax.ShapeDtypeStruct((4, 4) + policy_key.shape, policy_key.dtype),
        ),
        in_specs=[pl.BlockSpec(memory_space=pltpu.VMEM)] * 8,
        out_specs=(any_space, any_space),
        scratch_shapes=[
            pltpu.VMEM((4, rows, depth), tokens.dtype),
            pltpu.VMEM((4, 4 * block, width), ref_qkv.dtype),
            pltpu.VMEM((rows, width), jnp.float32),
            pltpu.VMEM((rows, HD), jnp.bfloat16),
            pltpu.VMEM((rows, HD), jnp.bfloat16),
            pltpu.VMEM((4, mine, share * HD), jnp.bfloat16),
            pltpu.SemaphoreType.DMA((N_COPIES,)),
            pltpu.SemaphoreType.DMA((N_COPIES,)),
            pltpu.SemaphoreType.DMA((3,)),
            pltpu.SemaphoreType.DMA((4,)),
            pltpu.SemaphoreType.DMA((4,)),
        ],
        compiler_params=pltpu.CompilerParams(
            collective_id=0, has_side_effects=True, vmem_limit_bytes=60 * 1024 * 1024
        ),
    )(tokens, ref_qkv, bias, cosine, sine, seg[:, None], seg[None, :], policy_key)
    return out, pg.reshape((-1,) + policy_key.shape[1:])


def per_group(tokens, ref_qkv, ref_bias, segment_ids, policy_key):
    rank = lax.axis_index("rep")
    width = ref_qkv.shape[1] // 4
    bias = lax.dynamic_slice_in_dim(ref_bias, rank * width, width, 0)[None, :]
    seg = segment_ids[0]
    pos = positions_of(seg)
    half = HD // 2
    freq = 1000000.0 ** (-2.0 * jnp.arange(half, dtype=jnp.float32) / HD)
    angle = pos.astype(jnp.float32)[:, None] * freq[None, :]
    cosine, sine = jnp.cos(angle), jnp.sin(angle)
    cosine = jnp.concatenate([cosine, cosine], axis=-1)
    sine = jnp.concatenate([-sine, sine], axis=-1)
    return whole_layer(tokens, ref_qkv, bias, cosine, sine, seg, policy_key)


def solution(mesh):
    in_specs = (
        P("fsdp", "rep"),
        P(("rep", "fsdp"), "tp"),
        P("tp"),
        P("fsdp", None),
        P(("rep", "fsdp"), "tp"),
    )
    out_specs = (P(("fsdp", "rep"), "tp"), P(None, "tp"))
    shape = mesh.shape
    grouped = (
        shape["rep"] == 4 and shape["fsdp"] == 4 and shape["tp"] == 2 and KVH == shape["tp"] * shape["rep"]
    )
    return jax.shard_map(
        per_group if grouped else per_device, mesh=mesh, in_specs=in_specs, out_specs=out_specs, check_vma=False
    )
```

profile of v0, /device:TPU:0, one launch (start us, length us, event | category | flops | bytes accessed | tf_op | source)
XLA Modules:
  0.0 209.5 jit_solution(9785624281968355094)
XLA Ops:
  0.6 0.9 compare_reduce_fusion
  1.5 0.1 add_select_fusion
  1.6 0.3 reduce-window.9
  1.9 0.8 dynamic_slice.3
  2.6 0.6 broadcast_in_dim.9.bias
  3.2 0.1 slice.17
  3.3 0.1 slice_reduce_fusion
  3.5 0.1 fusion.1
  3.5 1.7 copy.7.seg_col
  5.2 1.9 fusion
  7.2 1.3 pad_maximum_fusion
  8.5 193.3 %shard_map.68 = (bf16[256,2560]{1,0:T(8,128)(2,1)}, bf16[4,4,320,512]{3,2,1,0:T(8,128)(2,1)}) custom-call(bf16[1024,1280]{1,0:T(8,128)(2,1)} %tok.1, bf16[320,3584]{1,0:T(8,128)(2,1)} %w.1, f32[1,896]{1,0:T(1,128)} %broadcast_in_dim.9.bias, f32[1024,128]{1,0:T(8,128)} %get-tuple-element.9.cosine, f32[1024,128]{1,0:T(8,128)} %get-tuple-element.10.sine, ...), custom_call_target="tpu_custom_call" | custom-call | tf_op jit(solution)/shard_map/pallas_call | solution.py:360
  201.8 2.5 %copy.10 = bf16[256,2560]{1,0:T(8,128)(2,1)} copy(bf16[256,2560]{1,0:T(8,128)(2,1)} %get-tuple-element.13) | data formatting | bytes 2621440
  204.3 5.2 %copy.11 = bf16[5120,512]{1,0:T(8,128)(2,1)} copy(bf16[5120,512]{1,0:T(8,128)(2,1)} %bitcast.10) | data formatting | bytes 10485760
  (2 shorter events, 0.0 us)
where the time goes:
time: 211 us; the launch traced here: 209 us
  Pallas kernels  193 us (91%)
  local copies, waits for them, and re-layouts  10.9 us (5%)
  other arithmetic  4.53 us (2%)
    pallas_call x1, Pallas kernels, whole_layer(): pl.pallas_call(layer_kernel, out_shape=(jax.ShapeDtypeStruct((mine, 4 * s...  193 us
    unnamed x2, local copies, waits for them, and re-layouts  7.64 us

commit v1 on v0

v1 whole, which is shorter than its diff:
```python
import jax
import jax.numpy as jnp
from jax import lax
from jax.experimental import pallas as pl
from jax.experimental.pallas import tpu as pltpu
from jax.sharding import PartitionSpec as P
import functools
import math

MESH = pl.DeviceIdType.MESH

QH = 40
KVH = 8
HD = 128


def positions_of(seg):
    count = seg.shape[0]
    index = jnp.arange(count, dtype=jnp.int32)
    starts = jnp.concatenate([jnp.ones((1,), bool), seg[1:] != seg[:-1]])
    first = lax.cummax(jnp.where(starts, index, 0), axis=0)
    return index - first


def rotary(values, pos):
    half = values.shape[-1] // 2
    freq = 1000000.0 ** (-2.0 * jnp.arange(half, dtype=jnp.float32) / values.shape[-1])
    angle = pos.astype(jnp.float32)[:, None] * freq[None, :]
    shape = (values.shape[0],) + (1,) * (values.ndim - 2) + (half,)
    cosine = jnp.cos(angle).reshape(shape)
    sine = jnp.sin(angle).reshape(shape)
    first = values[..., :half]
    second = values[..., half:]
    return jnp.concatenate(
        [first * cosine - second * sine, second * cosine + first * sine], axis=-1
    )


def per_device(tokens, ref_qkv, ref_bias, segment_ids, policy_key):
    share = QH // KVH
    rows = tokens.shape[0]
    columns = ref_qkv.shape[1]
    groups = columns // ((share + 2) * HD)
    replicas = lax.axis_size("rep")
    mine = rows // replicas
    rank = lax.axis_index("rep")
    partial_value = jnp.dot(
        tokens,
        lax.all_gather(ref_qkv, "fsdp", axis=0, tiled=True),
        preferred_element_type=jnp.float32,
    )
    partial_value = partial_value.reshape(rows, groups, share + 2, HD)
    bias = ref_bias.reshape(groups, share + 2, HD)
    seg = segment_ids[0]
    pos = positions_of(seg)
    start = rank * mine
    my_pos = lax.dynamic_slice_in_dim(pos, start, mine, 0)
    summed = lax.psum_scatter(partial_value, "rep", scatter_dimension=0, tiled=True) + bias[None]
    query = rotary(summed[:, :, :share], my_pos).astype(jnp.bfloat16)
    my_keys = rotary(summed[:, :, share], my_pos).astype(jnp.bfloat16)
    my_vals = summed[:, :, share + 1].astype(jnp.bfloat16)
    keys, vals = (
        lax.all_gather(my_keys, "rep", axis=0, tiled=True),
        lax.all_gather(my_vals, "rep", axis=0, tiled=True),
    )
    scores = jnp.einsum(
        "qhgd,khd->hgqk", query, keys, preferred_element_type=jnp.float32
    ) / jnp.sqrt(jnp.float32(HD))
    query_index = start + jnp.arange(mine, dtype=jnp.int32)
    key_index = jnp.arange(rows, dtype=jnp.int32)
    my_seg = lax.dynamic_slice_in_dim(seg, start, mine, 0)
    allowed = (my_seg[:, None] == seg[None, :]) & (key_index[None, :] <= query_index[:, None])
    scores = jnp.where(allowed[None, None], scores, -1e30)
    top = jnp.max(scores, axis=-1, keepdims=True)
    expo = jnp.exp(scores - top)
    weights = (expo / jnp.sum(expo, axis=-1, keepdims=True)).astype(jnp.bfloat16)
    context = jnp.einsum("hgqk,khd->qhgd", weights, vals, preferred_element_type=jnp.float32)
    context = context.astype(jnp.bfloat16).reshape(mine, groups * share * HD)
    inner = lax.all_gather(policy_key, "rep", axis=0, tiled=True)
    outer = lax.all_gather(inner, "fsdp", axis=0, tiled=True)
    blocks = policy_key.shape[0]
    shards = outer.shape[0] // (blocks * replicas)
    whole = (
        outer.reshape(shards, replicas, blocks, outer.shape[1])
        .transpose(1, 0, 2, 3)
        .reshape(outer.shape)
    )
    return (context, whole)


def greet(devices, extra, condition):
    barrier = pltpu.get_barrier_semaphore()
    for device in devices:
        pl.semaphore_signal(barrier, inc=1, device_id=device, device_id_type=MESH)

    @pl.when(condition)
    def _():
        pl.semaphore_signal(barrier, inc=1, device_id=extra, device_id_type=MESH)
        pl.semaphore_wait(barrier, len(devices) + 1)

    @pl.when(jnp.logical_not(condition))
    def _():
        pl.semaphore_wait(barrier, len(devices))


class Copies:
    def __init__(self, send, recv):
        self.send, self.recv, self.made = send, recv, []

    def make(self, src, dst, device, sends=None):
        n = len(self.made)
        copy = pltpu.make_async_remote_copy(
            src_ref=src, dst_ref=dst, send_sem=self.send.at[n], recv_sem=self.recv.at[n],
            device_id=device, device_id_type=MESH,
        )
        self.made.append((copy, sends))
        return copy

    def start(self, src, dst, device, sends=None):
        copy = self.make(src, dst, device, sends)
        only(sends, copy.start)
        return copy

    def finish(self):
        for copy, sends in self.made:
            only(sends, copy.wait_send)


def only(condition, act):
    if condition is None:
        act()
    else:
        pl.when(condition)(act)


N_COPIES = 62


def layer_kernel(
    tok, w, bias, freq, seg, pol, out, pg,
    x, wg, own, snd, inb, kv, shut, cosine, sine, ctx, pv,
    send, recv, w_local, local, z_send, z_recv,
):
    f, r, t = lax.axis_index("fsdp"), lax.axis_index("rep"), lax.axis_index("tp")
    mine = x.shape[0] // 4
    block, columns = w.shape
    hb = block // 2
    groups = columns // ((QH // KVH + 2) * HD)
    share = QH // KVH
    width = columns // groups
    fx = f + 1 - 2 * lax.rem(f, 2)
    fy = lax.rem(f + 2, 4)
    near = r + 1 - 2 * lax.rem(r, 2)
    across = 3 - r
    end = (r == 0) | (r == 3)
    mid = (r == 1) | (r == 2)
    to_x, to_y, to_near, to_across = {"fsdp": fx}, {"fsdp": fy}, {"rep": near}, {"rep": across}
    to_up, to_down = {"rep": lax.rem(r + 1, 4)}, {"rep": lax.rem(r + 3, 4)}
    copies = Copies(send, recv)

    chunks = [(g * width + share * HD, 2 * HD) for g in range(groups)]
    chunks += [(g * width, share * HD) for g in range(groups)]
    n = len(chunks)
    col = [pl.ds(at, wide) for at, wide in chunks]

    load_w = []
    my_rows = pl.ds(pl.multiple_of(f * block, 16), block)
    for c in range(n):
        load_w.append(pltpu.make_async_copy(w.at[:, col[c]], wg.at[my_rows, col[c]], w_local.at[c]))
        load_w[c].start()
    load_x = pltpu.make_async_copy(tok, x, local.at[0])
    load_p = pltpu.make_async_copy(pol, pv, local.at[1])
    load_p.start()
    load_x.start()
    greet([to_x, to_y, to_near], to_across, mid)

    def held(owner, first, count, c):
        return wg.at[pl.ds(pl.multiple_of(owner * block + first, 16), count), col[c]]

    passed, onwards = {}, {}

    def direct(c):
        load_w[c].wait()
        src = held(f, 0, block, c)
        passed[c] = copies.start(src, src, to_x), copies.start(src, src, to_y)

    def onward(c):
        bx, by = passed[c]
        bx.wait_recv()
        a = copies.start(held(fx, 0, hb, c), held(fx, 0, hb, c), to_y)
        by.wait_recv()
        b = copies.start(held(fy, hb, hb, c), held(fy, hb, hb, c), to_x)
        onwards[c] = a, b

    p_up, p_down = {}, {}

    def policy_z(k):
        up_block, down_block = lax.rem(r + 5 - k, 4), lax.rem(r + k - 1, 4)
        up_src = pv if k == 1 else pg.at[up_block, f]
        down_src = pv if k == 1 else pg.at[down_block, f]
        if k > 1:
            landed_z(k - 1)
        p_up[k] = copies.start(up_src, pg.at[up_block, f], to_up, (r <= 2) & (r >= k - 1))
        p_down[k] = copies.start(down_src, pg.at[down_block, f], to_down, (r >= 1) & (r <= 4 - k))

    def landed_z(k):
        only(r >= k, p_up[k].wait_recv)
        only(r <= 3 - k, p_down[k].wait_recv)

    p_direct, p_onward = {}, {}

    def policy_direct(j):
        src = pg.at[j, f]
        p_direct[j] = copies.start(src, src, to_x), copies.start(src, src, to_y)

    def policy_onward(j):
        top, low = pl.ds(0, hb), pl.ds(hb, hb)
        bx, by = p_direct[j]
        bx.wait_recv()
        a = copies.start(pg.at[j, fx, top], pg.at[j, fx, top], to_y)
        by.wait_recv()
        b = copies.start(pg.at[j, fy, low], pg.at[j, fy, low], to_x)
        p_onward[j] = a, b

    def rows_of(slot):
        ahead = jnp.where(
            slot == 0, 3, jnp.where(slot == 1, 2, jnp.where((slot == 2) == end, 1, 0))
        )
        return jnp.where(r >= 2, 3 - ahead, ahead)

    def partial(c):
        def one(slot, _):
            rows = pl.ds(pl.multiple_of(rows_of(slot) * mine, mine), mine)
            own[slot, :, col[c]] = jnp.dot(x[rows, :], wg[:, col[c]], preferred_element_type=jnp.float32)
            return 0

        lax.fori_loop(0, 4, one, 0)

    def hop(c, slot, place, device):
        return pltpu.make_async_remote_copy(
            src_ref=snd.at[slot, :, col[c]], dst_ref=inb.at[place, :, col[c]],
            send_sem=z_send.at[slot, c], recv_sem=z_recv.at[place, c],
            device_id=device, device_id_type=MESH,
        )

    def came(c, place):
        hop(c, 0, place, to_near).wait_recv()

    def send_from_end(c):
        for slot in range(3):
            snd[slot, :, col[c]] = own[slot, :, col[c]].astype(jnp.bfloat16)
            hop(c, slot, slot, to_near).start()

    def send_from_mid(c):
        for slot, source, place, device in ((0, 0, 3, to_across), (2, 3, 2, to_near), (1, 1, 4, to_across)):
            came(c, source)
            total = own[slot, :, col[c]] + inb[source, :, col[c]].astype(jnp.float32)
            snd[slot, :, col[c]] = total.astype(jnp.bfloat16)
            hop(c, slot, place, device).start()

    def arrive(c):
        came(c, 2)
        pl.when(mid)(lambda: came(c, 4))

    def summed(at):
        return (
            own[3, :, at] + inb[2, :, at].astype(jnp.float32)
            + inb[4, :, at].astype(jnp.float32) + bias[:, at]
        )

    def rotated(values):
        return values * cosine[...] + pltpu.roll(values, HD // 2, 1) * sine[...]

    kv_up, kv_on = {}, {}

    def key_columns(g):
        return pl.ds(g * 2 * HD, HD), pl.ds(g * 2 * HD + HD, HD), pl.ds(g * 2 * HD, 2 * HD)

    def finish_keys(g):
        arrive(g)
        at, _ = chunks[g]
        kc, vc, both = key_columns(g)
        kv[pl.ds(2 * mine, mine), kc] = rotated(summed(pl.ds(at, HD))).astype(jnp.bfloat16)
        kv[pl.ds(2 * mine, mine), vc] = summed(pl.ds(at + HD, HD)).astype(jnp.bfloat16)
        kv_up[g] = copies.start(
            kv.at[pl.ds(2 * mine, mine), both], kv.at[pl.ds(mine, mine), both], to_up, r <= 2
        )

    def forward_keys(g):
        _, _, both = key_columns(g)
        only(r >= 1, kv_up[g].wait_recv)
        kv_on[g] = copies.start(
            kv.at[pl.ds(mine, mine), both], kv.at[pl.ds(0, mine), both], to_up, mid
        )

    scale = 1.0 / math.sqrt(HD)
    outs = []

    def attend(g):
        c = groups + g
        arrive(c)
        only(r >= 2, kv_on[g].wait_recv)
        kc, vc, _ = key_columns(g)

        def head(j, _):
            at = pl.ds(pl.multiple_of(g * width + j * HD, HD), HD)
            query = rotated(summed(at)).astype(jnp.bfloat16)
            scores = lax.dot_general(
                query, kv[:, kc], (((1,), (1,)), ((), ())), preferred_element_type=jnp.float32
            ) * scale + shut[...]
            expo = jnp.exp(scores - jnp.max(scores, axis=-1, keepdims=True))
            total = jnp.sum(expo, axis=-1, keepdims=True)
            weights = (expo * (1.0 / total)).astype(jnp.bfloat16)
            to = pl.ds(pl.multiple_of((g * share + j) * HD, HD), HD)
            ctx[:, to] = jnp.dot(weights, kv[:, vc], preferred_element_type=jnp.float32).astype(jnp.bfloat16)
            return 0

        lax.fori_loop(0, share, head, 0)
        part = pl.ds(g * share * HD, share * HD)
        copy = pltpu.make_async_copy(ctx.at[:, part], out.at[:, part], local.at[3 + g])
        copy.start()
        outs.append(copy)

    def prepare():
        at = pl.ds(pl.multiple_of(r * mine, mine), mine)
        square = (mine, mine)
        row, lane = lax.broadcasted_iota(jnp.int32, square, 0), lax.broadcasted_iota(jnp.int32, square, 1)
        mine_row = jnp.broadcast_to(seg[:, at].astype(jnp.float32), square)
        my_seg = jnp.sum(jnp.where(row == lane, mine_row, 0.0), axis=-1, keepdims=True)
        before = jnp.where(seg[...].astype(jnp.float32) < my_seg, 1.0, 0.0)
        first = jnp.sum(before, axis=-1, keepdims=True)
        index = lax.broadcasted_iota(jnp.int32, (mine, HD), 0) + r * mine
        angle = (index.astype(jnp.float32) - first) * freq[...]
        half = lax.broadcasted_iota(jnp.int32, (mine, HD), 1) < HD // 2
        cosine[...] = jnp.cos(angle)
        wave = jnp.sin(angle)
        sine[...] = jnp.where(half, -wave, wave)
        for slot in range(3):
            there = r - 2 + slot
            keys = pl.ds(pl.multiple_of(jnp.maximum(there, 0) * mine, mine), mine)
            allowed = (my_seg == seg[:, keys].astype(jnp.float32)) & (there >= 0)
            if slot == 2:
                allowed = allowed & (lane <= row)
            shut[:, slot * mine:(slot + 1) * mine] = jnp.where(allowed, 0.0, -1e30)

        @pl.when(r <= 1)
        def _():
            kv[pl.ds(0, mine), :] = jnp.zeros((mine, kv.shape[1]), kv.dtype)

        @pl.when(r == 0)
        def _():
            kv[pl.ds(mine, mine), :] = jnp.zeros((mine, kv.shape[1]), kv.dtype)

        @pl.when(end)
        def _():
            inb[4] = jnp.zeros(inb.shape[1:], inb.dtype)

    direct(0)
    direct(1)
    load_p.wait()
    policy_z(1)
    keep_p = pltpu.make_async_copy(pv, pg.at[r, f], local.at[2])
    keep_p.start()
    onward(0)
    direct(2)
    onward(1)
    direct(3)
    load_x.wait()
    for c in range(n):
        for copy in onwards[c]:
            copy.wait_recv()
        partial(c)
        pl.when(end)(functools.partial(send_from_end, c))
        if c + 2 < n:
            onward(c + 2)
        if c + 4 < n:
            direct(c + 4)
        if c == 0:
            prepare()
            policy_z(2)
        if c == 1:
            policy_z(3)
        if c == 4:
            landed_z(3)
            keep_p.wait()
            policy_direct(0)
            policy_direct(1)
        if c == 6:
            policy_onward(0)
            policy_direct(2)
            policy_onward(1)
            policy_direct(3)
        pl.when(mid)(functools.partial(send_from_mid, c))
        if c == groups + 1:
            for g in range(groups):
                forward_keys(g)
        if 1 <= c <= groups:
            finish_keys(c - 1)
        if c > groups:
            attend(c - 1 - groups)
    policy_onward(2)
    policy_onward(3)
    attend(groups - 1)
    for copy in outs:
        copy.wait()
    for j in range(4):
        for copy in p_onward[j]:
            copy.wait_recv()
    for c in range(n):
        for slot in range(3):
            hop(c, slot, 0, to_near).wait_send()
    copies.finish()


def whole_layer(tokens, ref_qkv, ref_bias, segment_ids, policy_key):
    rows, depth = tokens.shape
    block, columns = ref_qkv.shape
    mine, share = rows // 4, QH // KVH
    groups = columns // ((share + 2) * HD)
    chunks = 2 * groups
    half = HD // 2
    freq = 1000000.0 ** (-2.0 * jnp.arange(half, dtype=jnp.float32) / HD)
    freq = jnp.concatenate([freq, freq])[None, :]
    any_space, vmem = pl.BlockSpec(memory_space=pl.ANY), pl.BlockSpec(memory_space=pltpu.VMEM)
    low, full = jnp.bfloat16, jnp.float32
    dma = pltpu.SemaphoreType.DMA
    out, pg = pl.pallas_call(
        layer_kernel,
        out_shape=(
            jax.ShapeDtypeStruct((mine, groups * share * HD), low),
            jax.ShapeDtypeStruct((4, 4) + policy_key.shape, policy_key.dtype),
        ),
        in_specs=[any_space, any_space, vmem, vmem, vmem, any_space],
        out_specs=(any_space, any_space),
        scratch_shapes=[
            pltpu.VMEM((rows, depth), tokens.dtype),
            pltpu.VMEM((4 * block, columns), ref_qkv.dtype),
            pltpu.VMEM((4, mine, columns), full),
            pltpu.VMEM((3, mine, columns), low),
            pltpu.VMEM((5, mine, columns), low),
            pltpu.VMEM((3 * mine, groups * 2 * HD), low),
            pltpu.VMEM((mine, 3 * mine), full),
            pltpu.VMEM((mine, HD), full),
            pltpu.VMEM((mine, HD), full),
            pltpu.VMEM((mine, groups * share * HD), low),
            pltpu.VMEM(policy_key.shape, policy_key.dtype),
            dma((N_COPIES,)),
            dma((N_COPIES,)),
            dma((chunks,)),
            dma((3 + groups,)),
            dma((3, chunks)),
            dma((5, chunks)),
        ],
        compiler_params=pltpu.CompilerParams(
            collective_id=0, has_side_effects=True, vmem_limit_bytes=60 * 1024 * 1024
        ),
    )(tokens, ref_qkv, ref_bias[None, :], freq, segment_ids, policy_key)
    return out, pg.reshape((-1,) + policy_key.shape[1:])


def solution(mesh):
    in_specs = (
        P("fsdp", "rep"),
        P(("rep", "fsdp"), "tp"),
        P("tp"),
        P("fsdp", None),
        P(("rep", "fsdp"), "tp"),
    )
    out_specs = (P(("fsdp", "rep"), "tp"), P(None, "tp"))
    shape = mesh.shape
    grouped = shape["rep"] == 4 and shape["fsdp"] == 4 and shape["tp"] == 2
    return jax.shard_map(
        whole_layer if grouped else per_device, mesh=mesh, in_specs=in_specs, out_specs=out_specs, check_vma=False
    )
```

time: 211 us -> 172 us (0.82)
  Pallas kernels: 193 us -> 161 us
  other arithmetic: 4.53 us -> 0.6 us
    pallas_call x1, Pallas kernels: 193 us -> 161 us  [whole_layer(): pl.pallas_call(layer_kernel, out_shape=(jax.ShapeDtypeStruct((mine, group...]
where the time goes in v1:
time: 172 us; the launch traced here: 171 us
  Pallas kernels  161 us (94%)
  local copies, waits for them, and re-layouts  8.96 us (5%)
    pallas_call x1, Pallas kernels, whole_layer(): pl.pallas_call(layer_kernel, out_shape=(jax.ShapeDtypeStruct((mine, group...  161 us
    unnamed x2, local copies, waits for them, and re-layouts  7.64 us

profile of v1, /device:TPU:0, one launch (start us, length us, event | category | flops | bytes accessed | tf_op | source)
XLA Modules:
  0.0 171.4 jit_solution(7677905646951801371)
XLA Ops:
  0.6 0.6 maximum_bitcast_fusion.freq
  1.2 1.3 broadcast_in_dim.6.bias
  2.6 161.2 %shard_map.68 = (bf16[256,2560]{1,0:T(8,128)(2,1)}, bf16[4,4,320,512]{3,2,1,0:T(8,128)(2,1)}) custom-call(bf16[1024,1280]{1,0:T(8,128)(2,1)} %tok.1, bf16[320,3584]{1,0:T(8,128)(2,1)} %w.1, f32[1,3584]{1,0:T(1,128)} %broadcast_in_dim.6.bias, f32[1,128]{1,0:T(1,128)} %maximum_bitcast_fusion.freq, s32[1,1024]{1,0:T(1,128)} %seg.1, bf16[320,512]{1,0:T(8,128)(2,1)} %pol.1), custom_call_target="tpu_custom_call" | custom-call | tf_op jit(solution)/shard_map/pallas_call | solution.py:427
  163.8 2.5 %copy.9 = bf16[256,2560]{1,0:T(8,128)(2,1)} copy(bf16[256,2560]{1,0:T(8,128)(2,1)} %get-tuple-element.8) | data formatting | bytes 2621440
  166.2 5.2 %copy.10 = bf16[5120,512]{1,0:T(8,128)(2,1)} copy(bf16[5120,512]{1,0:T(8,128)(2,1)} %bitcast.3) | data formatting | bytes 10485760
  (1 shorter events, 0.0 us)

commit v2 on v1

v2 whole, which is shorter than its diff:
```python
import jax
import jax.numpy as jnp
from jax import lax
from jax.experimental import pallas as pl
from jax.experimental.pallas import tpu as pltpu
from jax.sharding import PartitionSpec as P
import functools
import math

MESH = pl.DeviceIdType.MESH

QH = 40
KVH = 8
HD = 128


def positions_of(seg):
    count = seg.shape[0]
    index = jnp.arange(count, dtype=jnp.int32)
    starts = jnp.concatenate([jnp.ones((1,), bool), seg[1:] != seg[:-1]])
    first = lax.cummax(jnp.where(starts, index, 0), axis=0)
    return index - first


def rotary(values, pos):
    half = values.shape[-1] // 2
    freq = 1000000.0 ** (-2.0 * jnp.arange(half, dtype=jnp.float32) / values.shape[-1])
    angle = pos.astype(jnp.float32)[:, None] * freq[None, :]
    shape = (values.shape[0],) + (1,) * (values.ndim - 2) + (half,)
    cosine = jnp.cos(angle).reshape(shape)
    sine = jnp.sin(angle).reshape(shape)
    first = values[..., :half]
    second = values[..., half:]
    return jnp.concatenate(
        [first * cosine - second * sine, second * cosine + first * sine], axis=-1
    )


def per_device(tokens, ref_qkv, ref_bias, segment_ids, policy_key):
    share = QH // KVH
    rows = tokens.shape[0]
    columns = ref_qkv.shape[1]
    groups = columns // ((share + 2) * HD)
    replicas = lax.axis_size("rep")
    mine = rows // replicas
    rank = lax.axis_index("rep")
    partial_value = jnp.dot(
        tokens,
        lax.all_gather(ref_qkv, "fsdp", axis=0, tiled=True),
        preferred_element_type=jnp.float32,
    )
    partial_value = partial_value.reshape(rows, groups, share + 2, HD)
    bias = ref_bias.reshape(groups, share + 2, HD)
    seg = segment_ids[0]
    pos = positions_of(seg)
    start = rank * mine
    my_pos = lax.dynamic_slice_in_dim(pos, start, mine, 0)
    summed = lax.psum_scatter(partial_value, "rep", scatter_dimension=0, tiled=True) + bias[None]
    query = rotary(summed[:, :, :share], my_pos).astype(jnp.bfloat16)
    my_keys = rotary(summed[:, :, share], my_pos).astype(jnp.bfloat16)
    my_vals = summed[:, :, share + 1].astype(jnp.bfloat16)
    keys, vals = (
        lax.all_gather(my_keys, "rep", axis=0, tiled=True),
        lax.all_gather(my_vals, "rep", axis=0, tiled=True),
    )
    scores = jnp.einsum(
        "qhgd,khd->hgqk", query, keys, preferred_element_type=jnp.float32
    ) / jnp.sqrt(jnp.float32(HD))
    query_index = start + jnp.arange(mine, dtype=jnp.int32)
    key_index = jnp.arange(rows, dtype=jnp.int32)
    my_seg = lax.dynamic_slice_in_dim(seg, start, mine, 0)
    allowed = (my_seg[:, None] == seg[None, :]) & (key_index[None, :] <= query_index[:, None])
    scores = jnp.where(allowed[None, None], scores, -1e30)
    top = jnp.max(scores, axis=-1, keepdims=True)
    expo = jnp.exp(scores - top)
    weights = (expo / jnp.sum(expo, axis=-1, keepdims=True)).astype(jnp.bfloat16)
    context = jnp.einsum("hgqk,khd->qhgd", weights, vals, preferred_element_type=jnp.float32)
    context = context.astype(jnp.bfloat16).reshape(mine, groups * share * HD)
    inner = lax.all_gather(policy_key, "rep", axis=0, tiled=True)
    outer = lax.all_gather(inner, "fsdp", axis=0, tiled=True)
    blocks = policy_key.shape[0]
    shards = outer.shape[0] // (blocks * replicas)
    whole = (
        outer.reshape(shards, replicas, blocks, outer.shape[1])
        .transpose(1, 0, 2, 3)
        .reshape(outer.shape)
    )
    return (context, whole)


def greet(devices, extra, condition):
    barrier = pltpu.get_barrier_semaphore()
    for device in devices:
        pl.semaphore_signal(barrier, inc=1, device_id=device, device_id_type=MESH)

    @pl.when(condition)
    def _():
        pl.semaphore_signal(barrier, inc=1, device_id=extra, device_id_type=MESH)
        pl.semaphore_wait(barrier, len(devices) + 1)

    @pl.when(jnp.logical_not(condition))
    def _():
        pl.semaphore_wait(barrier, len(devices))


class Copies:
    def __init__(self, send, recv, ring):
        self.send, self.recv, self.ring = send, recv, ring
        self.made, self.done, self.left, self.used = [], 0, set(), 0

    def place(self):
        self.used += 1
        return self.used - 1

    def start(self, src, dst, device, sends=None, place=None):
        n = len(self.made)
        self.retire(n - self.ring + 1)
        place = self.place() if place is None else place
        copy = pltpu.make_async_remote_copy(
            src_ref=src, dst_ref=dst, send_sem=self.send.at[n % self.ring], recv_sem=self.recv.at[place],
            device_id=device, device_id_type=MESH,
        )
        only(sends, copy.start)
        self.made.append((copy, sends))
        return copy

    def arrival(self, ref, device, place):
        return pltpu.make_async_remote_copy(
            src_ref=ref, dst_ref=ref, send_sem=self.send.at[0], recv_sem=self.recv.at[place],
            device_id=device, device_id_type=MESH,
        )

    def sent(self, n):
        if n not in self.left:
            self.left.add(n)
            copy, sends = self.made[n]
            only(sends, copy.wait_send)

    def retire(self, count):
        while self.done < count:
            self.sent(self.done)
            self.done += 1


def only(condition, act):
    if condition is None:
        act()
    else:
        pl.when(condition)(act)


def sizes_of(g, groups, share):
    if g == groups - 1:
        return [2] * (share // 2) + [1] * (share % 2)
    return [share - share // 2, share // 2]


def plan(groups, share):
    width = (share + 2) * HD
    pieces = []
    for g in range(groups):
        pair = [("k", g, share), ("v", g, share + 1)]
        pieces += [pair[:1], pair[1:]] if g == 0 else [pair]
    for g in range(groups):
        at = 0
        for size in sizes_of(g, groups, share):
            pieces.append([("q", g, j) for j in range(at, at + size)])
            at += size
    return [(heads[0][1] * width + heads[0][2] * HD, heads) for heads in pieces]


def layer_kernel(
    tok, w, bias, seg, pol, out, pg,
    x, wg, own, fin, snd, inb, kv, shut, cosine, sine, ctx, pv,
    send, recv, w_local, local, z_send, z_recv,
):
    f, r, t = lax.axis_index("fsdp"), lax.axis_index("rep"), lax.axis_index("tp")
    mine = x.shape[0] // 4
    block, columns = w.shape
    hb = block // 2
    share = QH // KVH
    width = (share + 2) * HD
    groups = columns // width
    fx = f + 1 - 2 * lax.rem(f, 2)
    fy = lax.rem(f + 2, 4)
    near = r + 1 - 2 * lax.rem(r, 2)
    across = 3 - r
    end = (r == 0) | (r == 3)
    mid = (r == 1) | (r == 2)
    to_x, to_y, to_near, to_across = {"fsdp": fx}, {"fsdp": fy}, {"rep": near}, {"rep": across}
    to_up, to_down = {"rep": lax.rem(r + 1, 4)}, {"rep": lax.rem(r + 3, 4)}
    copies = Copies(send, recv, RING)

    chunks = plan(groups, share)
    n = len(chunks)
    wide = [len(heads) * HD for _, heads in chunks]
    col = [pl.ds(at, wide[c]) for c, (at, _) in enumerate(chunks)]

    my_rows = pl.ds(pl.multiple_of(f * block, 16), block)
    parts = col[:2] + [pl.ds(width, columns - width), pl.ds(0, share * HD)]
    load_w = [pltpu.make_async_copy(w.at[:, at], wg.at[my_rows, at], w_local.at[i]) for i, at in enumerate(parts)]
    for copy in load_w:
        copy.start()
    loaded = set()
    load_x = pltpu.make_async_copy(tok, x, local.at[0])
    load_p = pltpu.make_async_copy(pol, pv, local.at[1])
    load_p.start()
    load_x.start()
    greet([to_x, to_y, to_near], to_across, mid)

    def held(owner, first, count, c):
        return wg.at[pl.ds(pl.multiple_of(owner * block + first, 16), count), col[c]]

    passed, onwards, last_direct = {}, {}, {}

    def direct(c):
        part = c if c < 2 else (3 if chunks[c][0] < width else 2)
        if part not in loaded:
            loaded.add(part)
            load_w[part].wait()
        src = held(f, 0, block, c)
        place = copies.place()
        last_direct[c] = len(copies.made)
        copies.start(src, src, to_x, place=place)
        copies.start(src, src, to_y, place=place)
        passed[c] = copies.arrival(wg.at[pl.ds(0, 2 * block), col[c]], to_x, place)

    def left(c):
        copies.sent(last_direct[c])
        copies.sent(last_direct[c] + 1)

    def onward(c):
        passed[c].wait_recv()
        place = copies.place()
        copies.start(held(fx, 0, hb, c), held(fx, 0, hb, c), to_y, place=place)
        copies.start(held(fy, hb, hb, c), held(fy, hb, hb, c), to_x, place=place)
        onwards[c] = copies.arrival(wg.at[pl.ds(0, block), col[c]], to_x, place)

    def policy_at(j, owner, first=0, count=block):
        return pg.at[pl.ds(pl.multiple_of((j * 4 + owner) * block + first, 16), count)]

    p_up, p_down = {}, {}

    def policy_z(k):
        up_block, down_block = lax.rem(r + 5 - k, 4), lax.rem(r + k - 1, 4)
        up_src = pv if k == 1 else policy_at(up_block, f)
        down_src = pv if k == 1 else policy_at(down_block, f)
        if k > 1:
            landed_z(k - 1)
        p_up[k] = copies.start(up_src, policy_at(up_block, f), to_up, (r <= 2) & (r >= k - 1))
        p_down[k] = copies.start(down_src, policy_at(down_block, f), to_down, (r >= 1) & (r <= 4 - k))

    def landed_z(k):
        only(r >= k, p_up[k].wait_recv)
        only(r <= 3 - k, p_down[k].wait_recv)

    p_direct, p_onward = {}, {}

    def policy_direct(j):
        src, place = policy_at(j, f), copies.place()
        copies.start(src, src, to_x, place=place)
        copies.start(src, src, to_y, place=place)
        p_direct[j] = copies.arrival(pg.at[pl.ds(0, 2 * block)], to_x, place)

    def policy_onward(j):
        p_direct[j].wait_recv()
        place = copies.place()
        copies.start(policy_at(j, fx, 0, hb), policy_at(j, fx, 0, hb), to_y, place=place)
        copies.start(policy_at(j, fy, hb, hb), policy_at(j, fy, hb, hb), to_x, place=place)
        p_onward[j] = copies.arrival(pg.at[pl.ds(0, block)], to_x, place)

    def rows_of(slot):
        ahead = jnp.where(
            slot == 0, 3, jnp.where(slot == 1, 2, jnp.where((slot == 2) == end, 1, 0))
        )
        return jnp.where(r >= 2, 3 - ahead, ahead)

    def product(c, slot):
        rows = pl.ds(pl.multiple_of(rows_of(slot) * mine, mine), mine)
        return jnp.dot(x[rows, :], wg[:, col[c]], preferred_element_type=jnp.float32)

    def hop(c, slot, place, device):
        return pltpu.make_async_remote_copy(
            src_ref=snd.at[slot, :, col[c]], dst_ref=inb.at[place, :, col[c]],
            send_sem=z_send.at[slot, c % HOPS], recv_sem=z_recv.at[z_place(place), c],
            device_id=device, device_id_type=MESH,
        )

    def z_place(place):
        return (0, 1, 3, 2, 3)[place]

    def came(c, place):
        hop(c, 0, place, to_near).wait_recv()

    def came_last(c):
        both = inb.at[pl.ds(0, 2), :, col[c]]
        pair = pltpu.make_async_remote_copy(
            src_ref=both, dst_ref=both, send_sem=z_send.at[0, 0], recv_sem=z_recv.at[3, c],
            device_id=to_near, device_id_type=MESH,
        )
        pl.when(mid)(pair.wait_recv)
        pl.when(end)(hop(c, 0, 2, to_near).wait_recv)

    def work_end(c):
        def one(slot, _):
            snd[slot, :, col[c]] = product(c, slot).astype(jnp.bfloat16)
            pltpu.make_async_remote_copy(
                src_ref=snd.at[slot, :, col[c]], dst_ref=inb.at[slot, :, col[c]],
                send_sem=z_send.at[slot, c % HOPS], recv_sem=z_recv.at[jnp.where(slot == 2, 3, slot), c],
                device_id=to_near, device_id_type=MESH,
            ).start()
            return 0

        lax.fori_loop(0, 3, one, 0)
        fin[:, col[c]] = product(c, 3)

    def work_mid(c):
        here = pl.ds(0, wide[c])

        def one(slot, _):
            own[slot_of(c), slot, :, here] = product(c, slot)
            return 0

        lax.fori_loop(0, 3, one, 0)
        fin[:, col[c]] = product(c, 3)

    def work_one(c):
        if c >= 1:
            work_back(c - 1)
        if c == n - 1:
            work_back(c)
        work_across(c)

    def work_two(c):
        work_across(c)
        if c >= 1:
            work_back(c - 1)

    def work_across(c):
        relay(c, 0, 0, 3, to_across)
        relay(c, 1, 1, 4, to_across)

    def relay(c, slot, source, place, device):
        came(c, source)
        total = own[slot_of(c), slot, :, pl.ds(0, wide[c])] + inb[source, :, col[c]].astype(jnp.float32)
        snd[slot, :, col[c]] = total.astype(jnp.bfloat16)
        hop(c, slot, place, device).start()

    def work_back(c):
        relay(c, 2, 3, 2, to_near)

    def slot_of(c):
        return c % 2

    def summed(at):
        return (
            fin[:, at] + inb[2, :, at].astype(jnp.float32)
            + inb[4, :, at].astype(jnp.float32) + bias[at][None, :]
        )

    def rotated(values):
        return values * cosine[...] + pltpu.roll(values, HD // 2, 1) * sine[...]

    kv_up, kv_on = {}, {}

    def stored(kind, g):
        return pl.ds((2 * g + (kind == "v")) * HD, HD)

    def span(c):
        _, heads = chunks[c]
        return pl.ds((2 * heads[0][1] + (heads[0][0] == "v")) * HD, wide[c])

    key_chunks = [c for c in range(n) if chunks[c][1][0][0] != "q"]
    low, middle, high = (pl.ds(k * mine, mine) for k in range(3))

    def finish_keys(c):
        at, heads = chunks[c]
        for kind, g, j in heads:
            values = summed(pl.ds(at + (j - heads[0][2]) * HD, HD))
            kv[high, stored(kind, g)] = (rotated(values) if kind == "k" else values).astype(jnp.bfloat16)
        kv_up[c] = copies.start(kv.at[high, span(c)], kv.at[middle, span(c)], to_up, r <= 2)

    def forward_keys(c):
        only(r >= 1, kv_up[c].wait_recv)
        kv_on[c] = copies.start(kv.at[middle, span(c)], kv.at[low, span(c)], to_up, mid)

    scale = 1.0 / math.sqrt(HD)
    keys_in = set()

    def attend(c):
        at, heads = chunks[c]
        _, g, first = heads[0]
        for k in key_chunks:
            if k not in keys_in and chunks[k][1][0][1] == g:
                keys_in.add(k)
                only(r >= 2, kv_on[k].wait_recv)
        kc, vc = stored("k", g), stored("v", g)
        base = (g * share + first) * HD

        def head(j, _):
            query = rotated(summed(pl.ds(pl.multiple_of(at + j * HD, HD), HD))).astype(jnp.bfloat16)
            scores = lax.dot_general(
                query, kv[:, kc], (((1,), (1,)), ((), ())), preferred_element_type=jnp.float32
            ) * scale + shut[...]
            expo = jnp.exp(scores - jnp.max(scores, axis=-1, keepdims=True))
            total = jnp.sum(expo, axis=-1, keepdims=True)
            weights = (expo * (1.0 / total)).astype(jnp.bfloat16)
            to = pl.ds(pl.multiple_of(base + j * HD, HD), HD)
            ctx[:, to] = jnp.dot(weights, kv[:, vc], preferred_element_type=jnp.float32).astype(jnp.bfloat16)
            return 0

        lax.fori_loop(0, len(heads), head, 0)
        part = pl.ds(base, wide[c])
        pltpu.make_async_copy(ctx.at[:, part], out.at[:, part], local.at[3]).start()

    def finish(c):
        came_last(c)
        (attend if chunks[c][1][0][0] == "q" else finish_keys)(c)

    def prepare():
        at = pl.ds(pl.multiple_of(r * mine, mine), mine)
        square = (mine, mine)
        row, lane = lax.broadcasted_iota(jnp.int32, square, 0), lax.broadcasted_iota(jnp.int32, square, 1)
        mine_row = jnp.broadcast_to(seg[:, at].astype(jnp.float32), square)
        my_seg = jnp.sum(jnp.where(row == lane, mine_row, 0.0), axis=-1, keepdims=True)
        before = jnp.where(seg[...].astype(jnp.float32) < my_seg, 1.0, 0.0)
        first = jnp.sum(before, axis=-1, keepdims=True)
        index = lax.broadcasted_iota(jnp.int32, (mine, HD), 0) + r * mine
        half = HD // 2
        place = lax.rem(lax.broadcasted_iota(jnp.int32, (1, HD), 1), half)
        freq = jnp.ones((1, HD), jnp.float32)
        for i in range(1, half):
            freq = jnp.where(place == i, 1000000.0 ** (-2.0 * i / HD), freq)
        angle = (index.astype(jnp.float32) - first) * freq
        cosine[...] = jnp.cos(angle)
        wave = jnp.sin(angle)
        sine[...] = jnp.where(lax.broadcasted_iota(jnp.int32, (mine, HD), 1) < half, -wave, wave)
        for slot in range(3):
            there = r - 2 + slot
            keys = pl.ds(pl.multiple_of(jnp.maximum(there, 0) * mine, mine), mine)
            allowed = (my_seg == seg[:, keys].astype(jnp.float32)) & (there >= 0)
            if slot == 2:
                allowed = allowed & (lane <= row)
            shut[:, slot * mine:(slot + 1) * mine] = jnp.where(allowed, 0.0, -1e30)

        @pl.when(r <= 1)
        def _():
            kv[low, :] = jnp.zeros((mine, kv.shape[1]), kv.dtype)

        @pl.when(r == 0)
        def _():
            kv[middle, :] = jnp.zeros((mine, kv.shape[1]), kv.dtype)

        @pl.when(end)
        def _():
            inb[4] = jnp.zeros(inb.shape[1:], inb.dtype)

    def weights_in(c):
        onwards[c].wait_recv()

    queries = len(key_chunks)
    direct(0)
    load_p.wait()
    policy_z(1)
    keep_p = pltpu.make_async_copy(pv, policy_at(r, f), local.at[2])
    keep_p.start()
    left(0)
    direct(1)
    onward(0)
    direct(2)
    onward(1)
    direct(3)
    load_x.wait()
    weights_in(0)
    pl.when(end)(functools.partial(work_end, 0))
    onward(2)
    direct(4)
    prepare()
    policy_steps = {
        queries - 1: [("d", 0)], queries: [("d", 1)], queries + 1: [("o", 0), ("d", 2)], queries + 2: [("o", 1)],
        queries + 3: [("d", 3), ("o", 2)], queries + 5: [("o", 3)],
    }

    def weights_on(c):
        if c + 3 < n:
            onward(c + 3)
        if c + 5 < n:
            direct(c + 5)

    def sends_out(c):
        for slot in range(3):
            hop(c, slot, 0, to_near).wait_send()

    for c in range(n):
        if c + 1 >= HOPS:
            sends_out(c + 1 - HOPS)
        if 0 <= c - 4 < queries:
            forward_keys(c - 4)
        early = c - 2 < queries - 2
        if 0 <= c - 2 < queries and not early:
            finish(c - 2)
        if c + 1 < n:
            weights_in(c + 1)
            pl.when(end)(functools.partial(work_end, c + 1))
        if 0 <= c - 2 and early:
            finish(c - 2)
        if c < 3:
            weights_on(c)
        if c == 0:
            policy_z(2)
        if c == 2:
            policy_z(3)
        pl.when(mid)(functools.partial(work_mid, c))
        pl.when(r == 1)(functools.partial(work_one, c))
        pl.when(r == 2)(functools.partial(work_two, c))
        if c >= 3:
            weights_on(c)
        if c == queries - 1:
            landed_z(3)
            keep_p.wait()
        for kind, j in policy_steps.get(c, ()):
            (policy_direct if kind == "d" else policy_onward)(j)
        if queries <= c - 2 < n - 3:
            finish(c - 2)
        if c == n - 2:
            finish(c - 1)
    finish(n - 2)
    pl.when(r == 2)(functools.partial(work_back, n - 1))
    finish(n - 1)
    for j in range(4):
        p_onward[j].wait_recv()
    for c in range(n + 1 - HOPS, n):
        sends_out(c)
    copies.retire(len(copies.made))
    pltpu.make_async_copy(ctx, out, local.at[3]).wait()


def settle_kernel(ctx, pg, out, whole, ctx_held, pg_held, load, store):
    pieces = [(ctx, ctx_held, out, pl.ds(k * 128, 128)) for k in range(ctx.shape[0] // 128)]
    step = pg.shape[0] // 8
    pieces = [(pg, pg_held, whole, pl.ds(k * step, step)) for k in range(8)] + pieces
    loads = [
        pltpu.make_async_copy(src.at[at], held.at[at], load.at[i]) for i, (src, held, _, at) in enumerate(pieces)
    ]
    stores = [
        pltpu.make_async_copy(held.at[at], dst.at[at], store.at[i]) for i, (_, held, dst, at) in enumerate(pieces)
    ]
    for copy in loads:
        copy.start()
    for one, two in zip(loads, stores):
        one.wait()
        two.start()
    for copy in stores:
        copy.wait()


def whole_layer(tokens, ref_qkv, ref_bias, segment_ids, policy_key):
    rows, depth = tokens.shape
    block, columns = ref_qkv.shape
    mine, share = rows // 4, QH // KVH
    groups = columns // ((share + 2) * HD)
    chunks = plan(groups, share)
    n = len(chunks)
    keys = sum(heads[0][0] != "q" for _, heads in chunks)
    widest = max(len(heads) for _, heads in chunks) * HD
    places = 2 * n + 6 + 2 * keys + 8
    hbm, vmem = pl.BlockSpec(memory_space=pltpu.HBM), pl.BlockSpec(memory_space=pltpu.VMEM)
    any_space = pl.BlockSpec(memory_space=pl.ANY)
    low, full = jnp.bfloat16, jnp.float32
    dma = pltpu.SemaphoreType.DMA
    out, pg = pl.pallas_call(
        layer_kernel,
        out_shape=(
            jax.ShapeDtypeStruct((mine, groups * share * HD), low),
            jax.ShapeDtypeStruct((16 * block, policy_key.shape[1]), policy_key.dtype),
        ),
        in_specs=[hbm, hbm, vmem, vmem, hbm],
        out_specs=(any_space, any_space),
        scratch_shapes=[
            pltpu.VMEM((rows, depth), tokens.dtype),
            pltpu.VMEM((4 * block, columns), ref_qkv.dtype),
            pltpu.VMEM((2, 3, mine, widest), full),
            pltpu.VMEM((mine, columns), full),
            pltpu.VMEM((3, mine, columns), low),
            pltpu.VMEM((5, mine, columns), low),
            pltpu.VMEM((3 * mine, groups * 2 * HD), low),
            pltpu.VMEM((mine, 3 * mine), full),
            pltpu.VMEM((mine, HD), full),
            pltpu.VMEM((mine, HD), full),
            pltpu.VMEM((mine, groups * share * HD), low),
            pltpu.VMEM(policy_key.shape, policy_key.dtype),
            dma((RING,)),
            dma((places,)),
            dma((4,)),
            dma((4,)),
            dma((3, HOPS)),
            dma((4, n)),
        ],
        compiler_params=pltpu.CompilerParams(
            collective_id=0, has_side_effects=True, vmem_limit_bytes=VMEM_LIMIT
        ),
    )(tokens, ref_qkv, ref_bias, segment_ids, policy_key)
    pieces = 8 + mine // 128
    return pl.pallas_call(
        settle_kernel,
        out_shape=tuple(jax.ShapeDtypeStruct(a.shape, a.dtype) for a in (out, pg)),
        in_specs=[any_space] * 2,
        out_specs=(any_space,) * 2,
        scratch_shapes=[
            pltpu.VMEM(out.shape, out.dtype), pltpu.VMEM(pg.shape, pg.dtype), dma((pieces,)), dma((pieces,)),
        ],
        compiler_params=pltpu.CompilerParams(vmem_limit_bytes=VMEM_LIMIT),
    )(out, pg)


VMEM_LIMIT = 60 * 1024 * 1024
RING = 32
HOPS = 4


def solution(mesh):
    in_specs = (
        P("fsdp", "rep"),
        P(("rep", "fsdp"), "tp"),
        P("tp"),
        P("fsdp", None),
        P(("rep", "fsdp"), "tp"),
    )
    out_specs = (P(("fsdp", "rep"), "tp"), P(None, "tp"))
    shape = mesh.shape
    grouped = shape["rep"] == 4 and shape["fsdp"] == 4 and shape["tp"] == 2
    return jax.shard_map(
        whole_layer if grouped else per_device, mesh=mesh, in_specs=in_specs, out_specs=out_specs, check_vma=False
    )
```

time: 172 us -> 158 us (0.919)
  local copies, waits for them, and re-layouts: 8.96 us -> 0 us
  Pallas kernels: 161 us -> 157 us
    pallas_call x1, Pallas kernels: 161 us -> 151 us  [whole_layer(): pl.pallas_call(layer_kernel, out_shape=(jax.ShapeDtypeStruct((mine, group...]
    unnamed x2 -> x0, local copies, waits for them, and re-layouts: 7.64 us -> none
    pallas_call x0 -> x1, Pallas kernels: none -> 5.53 us  [whole_layer(): pl.pallas_call(settle_kernel, out_shape=tuple((jax.ShapeDtypeStruct(a.sha...]
where the time goes in v2:
time: 158 us
  Pallas kernels  157 us (99%)
    pallas_call x1, Pallas kernels, whole_layer(): pl.pallas_call(layer_kernel, out_shape=(jax.ShapeDtypeStruct((mine, group...  151 us
    pallas_call x1, Pallas kernels, whole_layer(): pl.pallas_call(settle_kernel, out_shape=tuple((jax.ShapeDtypeStruct(a.sha...  5.53 us

profile of v2, /device:TPU:0, one launch (start us, length us, event | category | flops | bytes accessed | tf_op | source)
XLA Modules:
  0.0 157.7 jit_solution(15943907284317058624)
XLA Ops:
  0.6 151.4 %shard_map.68 = (bf16[256,2560]{1,0:T(8,128)(2,1)}, bf16[5120,512]{1,0:T(8,128)(2,1)}) custom-call(bf16[1024,1280]{1,0:T(8,128)(2,1)} %tok.1, bf16[320,3584]{1,0:T(8,128)(2,1)} %w.1, f32[3584]{0:T(1024)} %bias.1, s32[1,1024]{1,0:T(1,128)} %seg.1, bf16[320,512]{1,0:T(8,128)(2,1)} %pol.1), custom_call_target="tpu_custom_call" | custom-call | tf_op jit(solution)/shard_map/pallas_call | solution.py:571
  152.0 5.5 %shard_map.69 = (bf16[256,2560]{1,0:T(8,128)(2,1)}, bf16[5120,512]{1,0:T(8,128)(2,1)}) custom-call(bf16[256,2560]{1,0:T(8,128)(2,1)} %get-tuple-element.4.ctx, bf16[5120,512]{1,0:T(8,128)(2,1)} %get-tuple-element.5.pg), custom_call_target="tpu_custom_call" | custom-call | tf_op jit(solution)/shard_map/pallas_call | solution.py:604

commit v3 on v2

--- a/solution.py
+++ b/solution.py
@@ -211,7 +211,7 @@
     def held(owner, first, count, c):
         return wg.at[pl.ds(pl.multiple_of(owner * block + first, 16), count), col[c]]
 
-    passed, onwards, last_direct = {}, {}, {}
+    passed, onwards, last_direct, last_onward = {}, {}, {}, {}
 
     def direct(c):
         part = c if c < 2 else (3 if chunks[c][0] < width else 2)
@@ -226,14 +226,15 @@
         passed[c] = copies.arrival(wg.at[pl.ds(0, 2 * block), col[c]], to_x, place)
 
     def left(c):
-        copies.sent(last_direct[c])
-        copies.sent(last_direct[c] + 1)
+        copies.sent(c)
+        copies.sent(c + 1)
 
     def onward(c):
         passed[c].wait_recv()
         place = copies.place()
         copies.start(held(fx, 0, hb, c), held(fx, 0, hb, c), to_y, place=place)
         copies.start(held(fy, hb, hb, c), held(fy, hb, hb, c), to_x, place=place)
+        last_onward[c] = len(copies.made) - 2
         onwards[c] = copies.arrival(wg.at[pl.ds(0, block), col[c]], to_x, place)
 
     def policy_at(j, owner, first=0, count=block):
@@ -325,11 +326,15 @@
         fin[:, col[c]] = product(c, 3)
 
     def work_one(c):
-        if c >= 1:
+        if 1 <= c <= n - 3:
             work_back(c - 1)
+        if c > n - 3:
+            work_back(c)
         if c == n - 1:
+            finish(n - 4)
+        work_across(c)
+        if c == n - 3:
             work_back(c)
-        work_across(c)
 
     def work_two(c):
         work_across(c)
@@ -464,11 +469,13 @@
     policy_z(1)
     keep_p = pltpu.make_async_copy(pv, policy_at(r, f), local.at[2])
     keep_p.start()
-    left(0)
+    left(last_direct[0])
     direct(1)
     onward(0)
+    left(last_onward[0])
     direct(2)
     onward(1)
+    left(last_onward[1])
     direct(3)
     load_x.wait()
     weights_in(0)
@@ -520,10 +527,11 @@
             keep_p.wait()
         for kind, j in policy_steps.get(c, ()):
             (policy_direct if kind == "d" else policy_onward)(j)
-        if queries <= c - 2 < n - 3:
+        if queries <= c - 2 < n - 4:
             finish(c - 2)
         if c == n - 2:
-            finish(c - 1)
+            pl.when(r != 1)(functools.partial(finish, n - 4))
+    finish(n - 3)
     finish(n - 2)
     pl.when(r == 2)(functools.partial(work_back, n - 1))
     finish(n - 1)
@@ -535,21 +543,12 @@
     pltpu.make_async_copy(ctx, out, local.at[3]).wait()
 
 
-def settle_kernel(ctx, pg, out, whole, ctx_held, pg_held, load, store):
-    pieces = [(ctx, ctx_held, out, pl.ds(k * 128, 128)) for k in range(ctx.shape[0] // 128)]
-    step = pg.shape[0] // 8
-    pieces = [(pg, pg_held, whole, pl.ds(k * step, step)) for k in range(8)] + pieces
-    loads = [
-        pltpu.make_async_copy(src.at[at], held.at[at], load.at[i]) for i, (src, held, _, at) in enumerate(pieces)
-    ]
-    stores = [
-        pltpu.make_async_copy(held.at[at], dst.at[at], store.at[i]) for i, (_, held, dst, at) in enumerate(pieces)
-    ]
-    for copy in loads:
+def settle_kernel(ctx, pg, out, whole, store):
+    step = pg.shape[0] // PIECES
+    stores = [(pg.at[pl.ds(k * step, step)], whole.at[pl.ds(k * step, step)]) for k in range(PIECES)] + [(ctx, out)]
+    stores = [pltpu.make_async_copy(src, dst, store.at[i]) for i, (src, dst) in enumerate(stores)]
+    for copy in stores:
         copy.start()
-    for one, two in zip(loads, stores):
-        one.wait()
-        two.start()
     for copy in stores:
         copy.wait()
 
@@ -571,8 +570,8 @@
     out, pg = pl.pallas_call(
         layer_kernel,
         out_shape=(
-            jax.ShapeDtypeStruct((mine, groups * share * HD), low),
-            jax.ShapeDtypeStruct((16 * block, policy_key.shape[1]), policy_key.dtype),
+            pltpu.VMEM((mine, groups * share * HD), low),
+            pltpu.VMEM((16 * block, policy_key.shape[1]), policy_key.dtype),
         ),
         in_specs=[hbm, hbm, vmem, vmem, hbm],
         out_specs=(any_space, any_space),
@@ -600,20 +599,18 @@
             collective_id=0, has_side_effects=True, vmem_limit_bytes=VMEM_LIMIT
         ),
     )(tokens, ref_qkv, ref_bias, segment_ids, policy_key)
-    pieces = 8 + mine // 128
     return pl.pallas_call(
         settle_kernel,
         out_shape=tuple(jax.ShapeDtypeStruct(a.shape, a.dtype) for a in (out, pg)),
         in_specs=[any_space] * 2,
         out_specs=(any_space,) * 2,
-        scratch_shapes=[
-            pltpu.VMEM(out.shape, out.dtype), pltpu.VMEM(pg.shape, pg.dtype), dma((pieces,)), dma((pieces,)),
-        ],
+        scratch_shapes=[dma((PIECES + 1,))],
         compiler_params=pltpu.CompilerParams(vmem_limit_bytes=VMEM_LIMIT),
-    )(out, pg)
-
-
-VMEM_LIMIT = 60 * 1024 * 1024
+    )(*(pltpu.with_memory_space_constraint(a, pltpu.VMEM) for a in (out, pg)))
+
+
+PIECES = 4
+VMEM_LIMIT = 50 * 1024 * 1024
 RING = 32
 HOPS = 4
 

time: 158 us -> 153 us (0.968); the launches traced: 158 us -> 151 us
  Pallas kernels: 157 us -> 150 us
    pallas_call x1, Pallas kernels: 151 us -> 147 us  [whole_layer(): pl.pallas_call(layer_kernel, out_shape=(pltpu.VMEM((mine, groups * share...]
    pallas_call x1, Pallas kernels: 5.53 us -> 2.83 us  [whole_layer(): pl.pallas_call(settle_kernel, out_shape=tuple((jax.ShapeDtypeStruct(a.sha...]
where the time goes in v3:
time: 153 us; the launch traced here: 151 us
  Pallas kernels  150 us (98%)
    pallas_call x1, Pallas kernels, whole_layer(): pl.pallas_call(layer_kernel, out_shape=(pltpu.VMEM((mine, groups * share...  147 us

profile of v3, /device:TPU:0, one launch (start us, length us, event | category | flops | bytes accessed | tf_op | source)
XLA Modules:
  0.0 150.7 jit_solution(8250997401594977736)
XLA Ops:
  0.6 147.1 %shard_map.68 = (bf16[256,2560]{1,0:T(8,128)(2,1)S(1)}, bf16[5120,512]{1,0:T(8,128)(2,1)S(1)}) custom-call(bf16[1024,1280]{1,0:T(8,128)(2,1)} %tok.1, bf16[320,3584]{1,0:T(8,128)(2,1)} %w.1, f32[3584]{0:T(1024)} %bias.1, s32[1,1024]{1,0:T(1,128)} %seg.1, bf16[320,512]{1,0:T(8,128)(2,1)} %pol.1), custom_call_target="tpu_custom_call" | custom-call | tf_op jit(solution)/shard_map/pallas_call | solution.py:570
  147.7 2.8 %shard_map.69 = (bf16[256,2560]{1,0:T(8,128)(2,1)}, bf16[5120,512]{1,0:T(8,128)(2,1)}) custom-call(bf16[256,2560]{1,0:T(8,128)(2,1)S(1)} %get-tuple-element.4.ctx, bf16[5120,512]{1,0:T(8,128)(2,1)S(1)} %get-tuple-element.5.pg), custom_call_target="tpu_custom_call" | custom-call | tf_op jit(solution)/shard_map/pallas_call | solution.py:602

commit v4 on v3

--- a/solution.py
+++ b/solution.py
@@ -302,18 +302,20 @@
         pl.when(mid)(pair.wait_recv)
         pl.when(end)(hop(c, 0, 2, to_near).wait_recv)
 
-    def work_end(c):
+    def work_end(*several):
         def one(slot, _):
-            snd[slot, :, col[c]] = product(c, slot).astype(jnp.bfloat16)
-            pltpu.make_async_remote_copy(
-                src_ref=snd.at[slot, :, col[c]], dst_ref=inb.at[slot, :, col[c]],
-                send_sem=z_send.at[slot, c % HOPS], recv_sem=z_recv.at[jnp.where(slot == 2, 3, slot), c],
-                device_id=to_near, device_id_type=MESH,
-            ).start()
+            for c in several:
+                snd[slot, :, col[c]] = product(c, slot).astype(jnp.bfloat16)
+                pltpu.make_async_remote_copy(
+                    src_ref=snd.at[slot, :, col[c]], dst_ref=inb.at[slot, :, col[c]],
+                    send_sem=z_send.at[slot, c % HOPS], recv_sem=z_recv.at[jnp.where(slot == 2, 3, slot), c],
+                    device_id=to_near, device_id_type=MESH,
+                ).start()
             return 0
 
         lax.fori_loop(0, 3, one, 0)
-        fin[:, col[c]] = product(c, 3)
+        for c in several:
+            fin[:, col[c]] = product(c, 3)
 
     def work_mid(c):
         here = pl.ds(0, wide[c])
@@ -326,12 +328,8 @@
         fin[:, col[c]] = product(c, 3)
 
     def work_one(c):
-        if 1 <= c <= n - 3:
+        if c >= 1:
             work_back(c - 1)
-        if c > n - 3:
-            work_back(c)
-        if c == n - 1:
-            finish(n - 4)
         work_across(c)
         if c == n - 3:
             work_back(c)
@@ -341,9 +339,23 @@
         if c >= 1:
             work_back(c - 1)
 
-    def work_across(c):
-        relay(c, 0, 0, 3, to_across)
-        relay(c, 1, 1, 4, to_across)
+    def work_across(*several):
+        for slot in range(2):
+            for c in several:
+                relay(c, slot, slot, 3 + slot, to_across)
+
+    def last_one():
+        work_back(n - 2)
+        work_back(n - 1)
+        work_across(n - 2, n - 1)
+
+    def last_two():
+        work_across(n - 2, n - 1)
+        work_back(n - 3)
+
+    def last_back():
+        work_back(n - 2)
+        work_back(n - 1)
 
     def relay(c, slot, source, place, device):
         came(c, source)
@@ -355,7 +367,7 @@
         relay(c, 2, 3, 2, to_near)
 
     def slot_of(c):
-        return c % 2
+        return c % 3
 
     def summed(at):
         return (
@@ -472,48 +484,46 @@
     left(last_direct[0])
     direct(1)
     onward(0)
-    left(last_onward[0])
-    direct(2)
     onward(1)
-    left(last_onward[1])
-    direct(3)
     load_x.wait()
     weights_in(0)
+    direct(2)
     pl.when(end)(functools.partial(work_end, 0))
-    onward(2)
-    direct(4)
-    prepare()
     policy_steps = {
         queries - 1: [("d", 0)], queries: [("d", 1)], queries + 1: [("o", 0), ("d", 2)], queries + 2: [("o", 1)],
         queries + 3: [("d", 3), ("o", 2)], queries + 5: [("o", 3)],
     }
 
+    weight_steps = {0: "o2 d3", 1: "o3 d4", 2: "o4 d5", 3: "o5 d6 d7", 4: "o6 o7 d8 d9"}
+
     def weights_on(c):
-        if c + 3 < n:
-            onward(c + 3)
-        if c + 5 < n:
-            direct(c + 5)
+        for word in weight_steps.get(c, f"o{c + 3} d{c + 5}").split():
+            if int(word[1:]) < n:
+                (direct if word[0] == "d" else onward)(int(word[1:]))
 
     def sends_out(c):
         for slot in range(3):
             hop(c, slot, 0, to_near).wait_send()
 
-    for c in range(n):
-        if c + 1 >= HOPS:
-            sends_out(c + 1 - HOPS)
+    for c in range(n - 2):
+        ahead = [c + 1] if c < n - 3 else [n - 2, n - 1]
+        for k in ahead:
+            if k >= HOPS:
+                sends_out(k - HOPS)
         if 0 <= c - 4 < queries:
             forward_keys(c - 4)
         early = c - 2 < queries - 2
         if 0 <= c - 2 < queries and not early:
             finish(c - 2)
-        if c + 1 < n:
-            weights_in(c + 1)
-            pl.when(end)(functools.partial(work_end, c + 1))
+        for k in ahead:
+            weights_in(k)
+        pl.when(end)(functools.partial(work_end, *ahead))
         if 0 <= c - 2 and early:
             finish(c - 2)
         if c < 3:
             weights_on(c)
         if c == 0:
+            prepare()
             policy_z(2)
         if c == 2:
             policy_z(3)
@@ -527,17 +537,20 @@
             keep_p.wait()
         for kind, j in policy_steps.get(c, ()):
             (policy_direct if kind == "d" else policy_onward)(j)
-        if queries <= c - 2 < n - 4:
+        if queries <= c - 2:
             finish(c - 2)
-        if c == n - 2:
-            pl.when(r != 1)(functools.partial(finish, n - 4))
+    for c in (n - 2, n - 1):
+        pl.when(mid)(functools.partial(work_mid, c))
+    pl.when(r == 1)(last_one)
+    pl.when(r == 2)(last_two)
+    finish(n - 4)
     finish(n - 3)
+    pl.when(r == 2)(last_back)
     finish(n - 2)
-    pl.when(r == 2)(functools.partial(work_back, n - 1))
     finish(n - 1)
     for j in range(4):
         p_onward[j].wait_recv()
-    for c in range(n + 1 - HOPS, n):
+    for c in range(n - HOPS, n):
         sends_out(c)
     copies.retire(len(copies.made))
     pltpu.make_async_copy(ctx, out, local.at[3]).wait()
@@ -578,7 +591,7 @@
         scratch_shapes=[
             pltpu.VMEM((rows, depth), tokens.dtype),
             pltpu.VMEM((4 * block, columns), ref_qkv.dtype),
-            pltpu.VMEM((2, 3, mine, widest), full),
+            pltpu.VMEM((3, 3, mine, widest), full),
             pltpu.VMEM((mine, columns), full),
             pltpu.VMEM((3, mine, columns), low),
             pltpu.VMEM((5, mine, columns), low),

time: 153 us -> 151 us (0.987)
  Pallas kernels: 150 us -> 147 us
    pallas_call x1, Pallas kernels: 147 us -> 145 us  [whole_layer(): pl.pallas_call(layer_kernel, out_shape=(pltpu.VMEM((mine, groups * share...]
where the time goes in v4:
time: 151 us; the launch traced here: 148 us
  Pallas kernels  147 us (97%)
    pallas_call x1, Pallas kernels, whole_layer(): pl.pallas_call(layer_kernel, out_shape=(pltpu.VMEM((mine, groups * share...  145 us

profile of v4, /device:TPU:0, one launch (start us, length us, event | category | flops | bytes accessed | tf_op | source)
XLA Modules:
  0.0 148.2 jit_solution(4066115016011682899)
XLA Ops:
  0.6 144.5 %shard_map.68 = (bf16[256,2560]{1,0:T(8,128)(2,1)S(1)}, bf16[5120,512]{1,0:T(8,128)(2,1)S(1)}) custom-call(bf16[1024,1280]{1,0:T(8,128)(2,1)} %tok.1, bf16[320,3584]{1,0:T(8,128)(2,1)} %w.1, f32[3584]{0:T(1024)} %bias.1, s32[1,1024]{1,0:T(1,128)} %seg.1, bf16[320,512]{1,0:T(8,128)(2,1)} %pol.1), custom_call_target="tpu_custom_call" | custom-call | tf_op jit(solution)/shard_map/pallas_call | solution.py:583
  145.2 2.8 %shard_map.69 = (bf16[256,2560]{1,0:T(8,128)(2,1)}, bf16[5120,512]{1,0:T(8,128)(2,1)}) custom-call(bf16[256,2560]{1,0:T(8,128)(2,1)S(1)} %get-tuple-element.4.ctx, bf16[5120,512]{1,0:T(8,128)(2,1)S(1)} %get-tuple-element.5.pg), custom_call_target="tpu_custom_call" | custom-call | tf_op jit(solution)/shard_map/pallas_call | solution.py:615

commit v5 on v4

--- a/solution.py
+++ b/solution.py
@@ -331,8 +331,6 @@
         if c >= 1:
             work_back(c - 1)
         work_across(c)
-        if c == n - 3:
-            work_back(c)
 
     def work_two(c):
         work_across(c)
@@ -347,7 +345,11 @@
     def last_one():
         work_back(n - 2)
         work_back(n - 1)
-        work_across(n - 2, n - 1)
+        relay(n - 2, 0, 0, 3, to_across)
+        relay(n - 1, 0, 0, 3, to_across)
+        finish(n - 4)
+        relay(n - 2, 1, 1, 4, to_across)
+        relay(n - 1, 1, 1, 4, to_across)
 
     def last_two():
         work_across(n - 2, n - 1)
@@ -530,6 +532,10 @@
         pl.when(mid)(functools.partial(work_mid, c))
         pl.when(r == 1)(functools.partial(work_one, c))
         pl.when(r == 2)(functools.partial(work_two, c))
+        if c == n - 3:
+            for k in ahead:
+                pl.when(mid)(functools.partial(work_mid, k))
+            pl.when(r == 1)(functools.partial(work_back, c))
         if c >= 3:
             weights_on(c)
         if c == queries - 1:
@@ -539,11 +545,9 @@
             (policy_direct if kind == "d" else policy_onward)(j)
         if queries <= c - 2:
             finish(c - 2)
-    for c in (n - 2, n - 1):
-        pl.when(mid)(functools.partial(work_mid, c))
     pl.when(r == 1)(last_one)
     pl.when(r == 2)(last_two)
-    finish(n - 4)
+    pl.when(r != 1)(functools.partial(finish, n - 4))
     finish(n - 3)
     pl.when(r == 2)(last_back)
     finish(n - 2)

time: 151 us -> 151 us (level)
  the two profiles are of different devices: /device:TPU:0 before, /device:TPU:26 now
where the time goes in v5:
time: 151 us; the launch traced here: 150 us
  Pallas kernels  150 us (99%)
    pallas_call x1, Pallas kernels, whole_layer(): pl.pallas_call(layer_kernel, out_shape=(pltpu.VMEM((mine, groups * share...  147 us

profile of v5, /device:TPU:26, one launch (start us, length us, event | category | flops | bytes accessed | tf_op | source)
XLA Modules:
  0.0 150.4 jit_solution(4612583641482803555)
XLA Ops:
  0.6 146.7 %shard_map.68 = (bf16[256,2560]{1,0:T(8,128)(2,1)S(1)}, bf16[5120,512]{1,0:T(8,128)(2,1)S(1)}) custom-call(bf16[1024,1280]{1,0:T(8,128)(2,1)} %tok.1, bf16[320,3584]{1,0:T(8,128)(2,1)} %w.1, f32[3584]{0:T(1024)} %bias.1, s32[1,1024]{1,0:T(1,128)} %seg.1, bf16[320,512]{1,0:T(8,128)(2,1)} %pol.1), custom_call_target="tpu_custom_call" | custom-call | tf_op jit(solution)/shard_map/pallas_call | solution.py:587
  147.4 2.8 %shard_map.69 = (bf16[256,2560]{1,0:T(8,128)(2,1)}, bf16[5120,512]{1,0:T(8,128)(2,1)}) custom-call(bf16[256,2560]{1,0:T(8,128)(2,1)S(1)} %get-tuple-element.4.ctx, bf16[5120,512]{1,0:T(8,128)(2,1)S(1)} %get-tuple-element.5.pg), custom_call_target="tpu_custom_call" | custom-call | tf_op jit(solution)/shard_map/pallas_call | solution.py:619

commit v6 on v5

--- a/solution.py
+++ b/solution.py
@@ -343,10 +343,10 @@
                 relay(c, slot, slot, 3 + slot, to_across)
 
     def last_one():
+        relay(n - 2, 0, 0, 3, to_across)
+        relay(n - 1, 0, 0, 3, to_across)
         work_back(n - 2)
         work_back(n - 1)
-        relay(n - 2, 0, 0, 3, to_across)
-        relay(n - 1, 0, 0, 3, to_across)
         finish(n - 4)
         relay(n - 2, 1, 1, 4, to_across)
         relay(n - 1, 1, 1, 4, to_across)

time: 151 us -> 149 us (0.987)
  the two profiles are of different devices: /device:TPU:26 before, /device:TPU:0 now
where the time goes in v6:
time: 149 us; the launch traced here: 147 us
  Pallas kernels  146 us (98%)
    pallas_call x1, Pallas kernels, whole_layer(): pl.pallas_call(layer_kernel, out_shape=(pltpu.VMEM((mine, groups * share...  143 us

profile of v6, /device:TPU:0, one launch (start us, length us, event | category | flops | bytes accessed | tf_op | source)
XLA Modules:
  0.0 147.1 jit_solution(6111155377081175838)
XLA Ops:
  0.6 143.5 %shard_map.68 = (bf16[256,2560]{1,0:T(8,128)(2,1)S(1)}, bf16[5120,512]{1,0:T(8,128)(2,1)S(1)}) custom-call(bf16[1024,1280]{1,0:T(8,128)(2,1)} %tok.1, bf16[320,3584]{1,0:T(8,128)(2,1)} %w.1, f32[3584]{0:T(1024)} %bias.1, s32[1,1024]{1,0:T(1,128)} %seg.1, bf16[320,512]{1,0:T(8,128)(2,1)} %pol.1), custom_call_target="tpu_custom_call" | custom-call | tf_op jit(solution)/shard_map/pallas_call | solution.py:587
  144.1 2.8 %shard_map.69 = (bf16[256,2560]{1,0:T(8,128)(2,1)}, bf16[5120,512]{1,0:T(8,128)(2,1)}) custom-call(bf16[256,2560]{1,0:T(8,128)(2,1)S(1)} %get-tuple-element.4.ctx, bf16[5120,512]{1,0:T(8,128)(2,1)S(1)} %get-tuple-element.5.pg), custom_call_target="tpu_custom_call" | custom-call | tf_op jit(solution)/shard_map/pallas_call | solution.py:619

commit v7 on v6

--- a/solution.py
+++ b/solution.py
@@ -545,6 +545,11 @@
             (policy_direct if kind == "d" else policy_onward)(j)
         if queries <= c - 2:
             finish(c - 2)
+    for j in range(4):
+        p_onward[j].wait_recv()
+    copies.retire(len(copies.made))
+    for c in range(n - HOPS, n - 3):
+        sends_out(c)
     pl.when(r == 1)(last_one)
     pl.when(r == 2)(last_two)
     pl.when(r != 1)(functools.partial(finish, n - 4))
@@ -552,11 +557,8 @@
     pl.when(r == 2)(last_back)
     finish(n - 2)
     finish(n - 1)
-    for j in range(4):
-        p_onward[j].wait_recv()
-    for c in range(n - HOPS, n):
+    for c in range(n - 3, n):
         sends_out(c)
-    copies.retire(len(copies.made))
     pltpu.make_async_copy(ctx, out, local.at[3]).wait()
 
 

time: 149 us -> 149 us (level)
  no operation moved by 1% of the time
where the time goes in v7:
time: 149 us; the launch traced here: 147 us
  Pallas kernels  146 us (98%)
    pallas_call x1, Pallas kernels, whole_layer(): pl.pallas_call(layer_kernel, out_shape=(pltpu.VMEM((mine, groups * share...  143 us

profile of v7, /device:TPU:0, one launch (start us, length us, event | category | flops | bytes accessed | tf_op | source)
XLA Modules:
  0.0 147.1 jit_solution(6162514275069318647)
XLA Ops:
  0.6 143.4 %shard_map.68 = (bf16[256,2560]{1,0:T(8,128)(2,1)S(1)}, bf16[5120,512]{1,0:T(8,128)(2,1)S(1)}) custom-call(bf16[1024,1280]{1,0:T(8,128)(2,1)} %tok.1, bf16[320,3584]{1,0:T(8,128)(2,1)} %w.1, f32[3584]{0:T(1024)} %bias.1, s32[1,1024]{1,0:T(1,128)} %seg.1, bf16[320,512]{1,0:T(8,128)(2,1)} %pol.1), custom_call_target="tpu_custom_call" | custom-call | tf_op jit(solution)/shard_map/pallas_call | solution.py:589
  144.1 2.8 %shard_map.69 = (bf16[256,2560]{1,0:T(8,128)(2,1)}, bf16[5120,512]{1,0:T(8,128)(2,1)}) custom-call(bf16[256,2560]{1,0:T(8,128)(2,1)S(1)} %get-tuple-element.4.ctx, bf16[5120,512]{1,0:T(8,128)(2,1)S(1)} %get-tuple-element.5.pg), custom_call_target="tpu_custom_call" | custom-call | tf_op jit(solution)/shard_map/pallas_call | solution.py:621
